TPU v7x, 32 devices: a whole 2x2x4 slice. The times are simulated.
32 devices in a mesh: row: 4 (over x, core), col: 2 (over y), depth: 4 (over z).
Axes of the slice: x: 2, y: 2, z: 4, core: 2. Of those that a mesh axis runs over, the one named last changes fastest.
Arguments:
- tokens: bfloat16 [2048, 8192], P('col', ('row', 'depth')), may hold values from -6 to 6
- weight: bfloat16 [8192, 24576], P(('row', 'depth'), 'col'), may hold values from -0.0625 to 0.0625
- prev_tokens: bfloat16 [2048, 8192], P('col', ('row', 'depth')), may hold values from -6 to 6
- prev_grad: bfloat16 [2048, 24576], P(('row', 'depth'), 'col'), may hold values from -0.3125 to 0.3125
Outputs:
- qkv: bfloat16 [2048, 24576], P(('row', 'depth'), 'col')
- weight_grad: float32 [8192, 24576], P(('row', 'depth'), 'col')
All inputs are finite; a program needn't handle non-finite values.
Results may differ from a plain program's by a relative error of at most 0.001.
Values may be sent and summed in bfloat16 or wider, within the bound.
A program may use at most 256 MiB of HBM per device.

v0:
```python
import jax
import jax.numpy as jnp
from jax import lax
from jax.sharding import PartitionSpec as P


def local(tokens, weight, prev_tokens, prev_grad):
    rows_of_weight = lax.all_gather(weight, "row", axis=0, tiled=True)
    gathered = lax.all_gather(tokens, "col", axis=0, tiled=True)
    mine = lax.all_to_all(gathered, "row", split_axis=0, concat_axis=1, tiled=True)
    prev_gathered = lax.all_gather(prev_tokens, "col", axis=0, tiled=True)
    summed = lax.psum_scatter(
        jnp.dot(mine, rows_of_weight, preferred_element_type=jnp.float32),
        "depth",
        scatter_dimension=0,
        tiled=True,
    )
    qkv = summed.astype(jnp.bfloat16)
    weight_grad = lax.dot_general(
        prev_gathered,
        lax.all_gather(prev_grad, ("row", "depth"), axis=0, tiled=True),
        (((0,), (0,)), ((), ())),
        preferred_element_type=jnp.float32,
    )
    return (qkv, weight_grad)


def solution(mesh):
    placed = (
        P("col", ("row", "depth")),
        P(("row", "depth"), "col"),
        P("col", ("row", "depth")),
        P(("row", "depth"), "col"),
    )
    return jax.shard_map(
        local,
        mesh=mesh,
        in_specs=placed,
        out_specs=(P(("row", "depth"), "col"), P(("row", "depth"), "col")),
        check_vma=False,
    )
```

profile of v0, /device:TPU:0, one launch (start us, length us, event | category | flops | bytes accessed | tf_op | source)
XLA Modules:
  0.0 1073.0 jit_solution(14860280853741704934)
XLA Ops:
  7.2 0.0 all-gather.5.cloned.1.call-start
  7.2 0.7 all-gather.5.cloned.1.call-update
  7.9 0.0 all-gather.7.cloned.1.call-start
  7.9 0.7 all-gather.7.cloned.1.call-update
  8.6 0.0 all-gather.9.cloned.1.call-start
  8.7 0.7 all-gather.9.cloned.1.call-update
  9.4 0.0 all-gather.11.cloned.1.call-start
  9.4 0.5 all-gather.11.cloned.1.call-update
  10.0 0.0 reduce-scatter.2.cloned.1.call-start
  10.0 35.4 %all-gather.5.cloned.1.call-done = bf16[2048,512]{1,0:T(8,128)(2,1)} async-done(((bf16[1024,512]{1,0:T(8,128)(2,1)}), bf16[2048,512]{1,0:T(8,128)(2,1)}) %all-gather.5.cloned.1.call-update) | async-done | bytes 2097168 | tf_op jit(solution)/shard_map/all_gather | solution.py:9
  45.4 33.6 %all_to_all.19 = bf16[4,512,512]{2,1,0:T(8,128)(2,1)S(1)} all-to-all(bf16[4,512,512]{2,1,0:T(8,128)(2,1)} %bitcast.8), channel_id=1, replica_groups=mesh['row'=4,'col'=2,'depth'=4] {'row'}, dimensions={0} | all-to-all | bytes 4194304 | tf_op jit(solution)/shard_map/all_to_all | solution.py:10
  79.0 2.4 copy.6
  81.3 266.6 %all-gather.7.cloned.1.call-done = bf16[2048,12288]{1,0:T(8,128)(2,1)} async-done(((bf16[512,12288]{1,0:T(8,128)(2,1)}), bf16[2048,12288]{1,0:T(8,128)(2,1)}) %all-gather.7.cloned.1.call-update) | async-done | bytes 50331664 | tf_op jit(solution)/shard_map/all_gather | solution.py:8
  347.9 36.7 %fusion = f32[512,12288]{1,0:T(8,128)} fusion(bf16[512,2048]{0,1:T(8,128)(2,1)} %bitcast.9, bf16[2048,12288]{1,0:T(8,128)(2,1)} %all-gather.7.cloned.1.call-done), kind=kOutput, calls=%fused_computation | convolution fusion | flops 25769803776 | bytes 77594624 | tf_op jit(solution)/shard_map/dot_general | solution.py:13
  384.6 0.0 reduce-scatter.2.cloned.1.call-update
  384.7 0.0 all-gather.9.cloned.1.call-done
  384.7 260.6 %all-gather.11.cloned.1.call-done = bf16[2048,12288]{1,0:T(8,128)(2,1)} async-done(((bf16[128,12288]{1,0:T(8,128)(2,1)}), bf16[2048,12288]{1,0:T(8,128)(2,1)}) %all-gather.11.cloned.1.call-update) | async-done | bytes 50331664 | tf_op jit(solution)/shard_map/all_gather | solution.py:21
  645.3 36.8 %fusion.1 = f32[512,12288]{1,0:T(8,128)} fusion(bf16[2048,512]{1,0:T(8,128)(2,1)} %all-gather.9.cloned.1.call-done, bf16[2048,12288]{1,0:T(8,128)(2,1)} %all-gather.11.cloned.1.call-done), kind=kOutput, calls=%fused_computation.1 | convolution fusion | flops 25769803776 | bytes 77594624 | tf_op jit(solution)/shard_map/dot_general | solution.py:19
  682.0 379.6 %reduce-scatter.2.cloned.1.call-done = f32[128,12288]{1,0:T(8,128)} async-done(((f32[512,12288]{1,0:T(8,128)}), f32[128,12288]{1,0:T(8,128)}) %reduce-scatter.2.cloned.1.call-update) | async-done | bytes 6291472 | tf_op jit(solution)/shard_map/reduce_scatter | solution.py:12
  1061.7 4.8 convert_element_type.3
Async XLA Ops:
  7.2 38.2 %all-gather.5.cloned.1.call-start = ((), (), s32[]{:S(2)}) async-start(), calls=%async_computation.2 | async-start | bytes 3145728 | tf_op jit(solution)/shard_map/all_gather | solution.py:9
  7.9 340.0 %all-gather.7.cloned.1.call-start = ((), (), s32[]{:S(2)}) async-start(), calls=%async_computation.3 | async-start | bytes 62914560 | tf_op jit(solution)/shard_map/all_gather | solution.py:8
  8.6 376.0 %all-gather.9.cloned.1.call-start = ((), (), s32[]{:S(2)}) async-start(), calls=%async_computation.5 | async-start | bytes 3145728 | tf_op jit(solution)/shard_map/all_gather | solution.py:11
  9.4 635.9 %all-gather.11.cloned.1.call-start = ((), (), s32[]{:S(2)}) async-start(), calls=%async_computation.6 | async-start | bytes 53477376 | tf_op jit(solution)/shard_map/all_gather | solution.py:21
  10.0 1051.7 %reduce-scatter.2.cloned.1.call-start = ((), (), s32[]{:S(2)}) async-start(), calls=%async_computation.4 | async-start | bytes 31457280 | tf_op jit(solution)/shard_map/reduce_scatter | solution.py:12
Sparse Core Ops, SparseCore 0:
  9.5 35.8 all-gather.4
  46.9 300.9 all-gather.6
  349.5 32.1 all-gather.8
  383.1 262.1 all-gather.10
  647.5 414.1 reduce-scatter.1
where the time goes:
time: 1070 us
  waiting for transfers between devices  945 us (88%)
  matrix products  73.5 us (7%)
  blocking collectives  33.6 us (3%)
  between operations  13.8 us (1%)
    reduce_scatter x1, waiting for transfers between devices, local(): lax.psum_scatter(jnp.dot(mine, rows_of_weight, preferred_element_type=jnp...  380 us
    all_gather x1, waiting for transfers between devices, local(): rows_of_weight = lax.all_gather(weight, 'row', axis=0, tiled=True)  267 us
    all_gather x1, waiting for transfers between devices, local(): lax.all_gather(prev_grad, ('row', 'depth'), axis=0, tiled=True)  261 us
    dot_general x1, matrix products, local(): lax.dot_general(prev_gathered, lax.all_gather(prev_grad, ('row', 'depth')...  36.8 us
    dot_general x1, matrix products, local(): jnp.dot(mine, rows_of_weight, preferred_element_type=jnp.float32)  36.7 us
    all_gather x1, waiting for transfers between devices, local(): gathered = lax.all_gather(tokens, 'col', axis=0, tiled=True)  35.4 us
    all_to_all x1, blocking collectives, local(): lax.all_to_all(gathered, 'row', split_axis=0, concat_axis=1, tiled=True)  33.6 us
  transfers between devices with their start and end apart: 5, of which 4 were waited for; matrix products, arithmetic and copies ran while one was open for 7% of the time, Pallas kernels for 0%

commit v1 on v0

v1 whole, which is shorter than its diff:
```python
import functools

import jax
import jax.numpy as jnp
from jax import lax
from jax.experimental import pallas as pl
from jax.experimental.pallas import tpu as pltpu
from jax.sharding import PartitionSpec as P

CC = 256
AHEAD = 8
RING = 8
PREFILL = 3
PIECES = 4
MESH = pl.DeviceIdType.MESH


def plain(tokens, weight, prev_tokens, prev_grad):
    rows_of_weight = lax.all_gather(weight, "row", axis=0, tiled=True)
    gathered = lax.all_gather(tokens, "col", axis=0, tiled=True)
    mine = lax.all_to_all(gathered, "row", split_axis=0, concat_axis=1, tiled=True)
    prev_gathered = lax.all_gather(prev_tokens, "col", axis=0, tiled=True)
    summed = lax.psum_scatter(
        jnp.dot(mine, rows_of_weight, preferred_element_type=jnp.float32),
        "depth",
        scatter_dimension=0,
        tiled=True,
    )
    weight_grad = lax.dot_general(
        prev_gathered,
        lax.all_gather(prev_grad, ("row", "depth"), axis=0, tiled=True),
        (((0,), (0,)), ((), ())),
        preferred_element_type=jnp.float32,
    )
    return (summed.astype(jnp.bfloat16), weight_grad)


def kernel(
    n, cols, carry,
    tokens, weight, grad,
    qkv, every, spread,
    tok, wslot, part, r1, r2, out,
    tok_local, tok_send, tok_recv, fan_send, fan_recv,
    w_send, w_recv, w_local,
    s1_send, s2_send, r1_recv, r2_recv,
    o_local, o_send, o_recv,
    g_send, g_recv, g_local, c_send, c_recv, x_send, x_recv, d_send, d_recv,
):
    row, col, z = lax.axis_index("row"), lax.axis_index("col"), lax.axis_index("depth")
    x, core = row // 2, row % 2
    half = n * CC
    own = grad.shape[0]
    piece = own // PIECES
    per_stage = PIECES + 1
    group = cols // 2
    local_rows = tokens.shape[0]
    in_half = lax.rem(col, group)
    holds = col // group == x
    end = (z == 0) | (z == 3)
    low = z < 2

    def flipped(m):
        a = core + (m % 2) - 2 * core * (m % 2)
        b = x + (m // 2) - 2 * x * (m // 2)
        return 2 * b + a

    near, over, cross = flipped(1), flipped(2), flipped(3)
    peers = {1: (near, col, z), 2: (over, col, z), 3: (cross, col, z)}

    def push(src, dst, ss, rs, to):
        return pltpu.make_async_remote_copy(src, dst, ss, rs, device_id=to, device_id_type=MESH)

    def w_copy(m, j):
        side = core if m == 2 else 1 - core
        at = pl.multiple_of(side * half + j * CC, CC)
        return push(weight.at[:, pl.ds(at, CC)], spread.at[j, m - 1], w_send.at[m - 1, j], w_recv.at[m - 1, j], peers[m])

    def w_loads(j):
        slot = lax.rem(j, 2)
        at = pl.multiple_of(core * half + j * CC, CC)
        rows = weight.shape[0]
        copies = [pltpu.make_async_copy(weight.at[:, pl.ds(at, CC)], wslot.at[slot, pl.ds(0, rows)], w_local.at[slot, 0])]
        for m in (1, 2, 3):
            copies.append(pltpu.make_async_copy(spread.at[j, m - 1], wslot.at[slot, pl.ds(m * rows, rows)], w_local.at[slot, m]))
        return copies

    def w_arrive(j):
        for m in (1, 2, 3):
            w_copy(m, j).wait_recv()
        for copy in w_loads(j):
            copy.start()

    def rows_of(r, d):
        return (r * 4 + d) * own

    def g_copy(way, s, q, to_next):
        step = 1 - 2 * way
        d = z - step * s
        to = (row, col, z + step) if to_next else (row, col, z)
        if q == PIECES:
            at = pl.ds(rows_of(over, d), carry)
            return push(every.at[at], every.at[at], g_send.at[way, s * per_stage + q], g_recv.at[way, s * per_stage + q], to)
        at = pl.ds(pl.multiple_of(rows_of(row, d) + q * piece, 16), piece)
        return push(every.at[at], every.at[at], g_send.at[way, s * per_stage + q], g_recv.at[way, s * per_stage + q], to)

    def g_own(way, q):
        step = 1 - 2 * way
        at = pl.ds(pl.multiple_of(rows_of(row, z) + q * piece, 16), piece)
        return push(grad.at[pl.ds(q * piece, piece)], every.at[at], g_send.at[way, q], g_recv.at[way, q], (row, col, z + step))

    def c_copy():
        return push(grad.at[pl.ds(0, carry)], every.at[pl.ds(rows_of(row, z), carry)], c_send.at[0], c_recv.at[0], peers[2])

    def c_landed():
        return push(grad.at[pl.ds(0, carry)], every.at[pl.ds(rows_of(over, z), carry)], c_send.at[0], c_recv.at[0], peers[2])

    def sends(way):
        return z < 3 if way == 0 else z > 0

    def has(way, s):
        return z >= s if way == 0 else z + s <= 3

    def g_recv_wait(way, s, q):
        step = 1 - 2 * way
        d = z - step * s
        if q == PIECES:
            at = pl.ds(rows_of(over, d), carry)
        else:
            at = pl.ds(pl.multiple_of(rows_of(row, d) + q * piece, 16), piece)
        index = (s - 1) * per_stage + q
        push(every.at[at], every.at[at], g_send.at[way, index], g_recv.at[way, index], (row, col, z)).wait_recv()

    def g_step(s, q):
        for way in (0, 1):
            if isinstance(s, int) and s == 0:
                if q < PIECES:
                    @pl.when(sends(way))
                    def _():
                        g_own(way, q).start()
                else:
                    @pl.when(sends(way))
                    def _():
                        g_copy(way, 0, q, True).start()
            else:
                @pl.when(has(way, s))
                def _():
                    g_recv_wait(way, s, q)

                    @pl.when(sends(way))
                    def _():
                        g_copy(way, s, q, True).start()

    def x_copy(d, i):
        rows = own - carry
        at = pl.ds(pl.multiple_of(rows_of(row, d) + carry, 16), rows)
        return push(every.at[at], every.at[at], x_send.at[i], x_recv.at[i], peers[2])

    def x_wait(d, i):
        rows = own - carry
        at = pl.ds(pl.multiple_of(rows_of(over, d) + carry, 16), rows)
        push(every.at[at], every.at[at], x_send.at[i], x_recv.at[i], peers[2]).wait_recv()

    def d_copy(r, d, i):
        at = pl.ds(pl.multiple_of(rows_of(r, d), 16), own)
        return push(every.at[at], every.at[at], d_send.at[i], d_recv.at[i], peers[1])

    def block_done(d):
        x_copy(d, d).start()
        d_copy(row, d, d).start()

    def stage_done(s):
        for way in (0, 1):
            step = 1 - 2 * way

            @pl.when(has(way, s))
            def _():
                block_done(z - step * s)

    def o_copies(j):
        slot = lax.rem(j, 4)
        at = pl.multiple_of(core * half + j * CC, CC)
        here = pltpu.make_async_copy(out.at[slot, core], qkv.at[:, pl.ds(at, CC)], o_local.at[slot])
        there = push(out.at[slot, 1 - core], qkv.at[:, pl.ds(at, CC)], o_send.at[slot], o_recv.at[j], peers[1])
        return here, there

    def o_wait(j):
        here, there = o_copies(j)
        here.wait()
        there.wait_send()

    def o_landed(j):
        slot = lax.rem(j, 4)
        at = pl.multiple_of((1 - core) * half + j * CC, CC)
        push(out.at[slot, core], qkv.at[:, pl.ds(at, CC)], o_send.at[slot], o_recv.at[j], peers[1]).wait_recv()

    def finish(j, value):
        @pl.when(j >= 4)
        def _():
            o_wait(j - 4)
        out[lax.rem(j, 4)] = value.astype(out.dtype)
        here, there = o_copies(j)
        here.start()
        there.start()

    def at_rows(a, b, size):
        return pl.ds(pl.multiple_of(jnp.where(low, a, b), own), size)

    def s1(j):
        slot = lax.rem(j, RING)
        return push(part.at[slot, :, at_rows(own, 0, 3 * own)], r1.at[j], s1_send.at[slot], r1_recv.at[j],
                    (row, col, jnp.where(low, 1, 2)))

    def s2(j):
        slot = lax.rem(j, RING)
        return push(part.at[slot, :, at_rows(2 * own, 0, 2 * own)], r2.at[j], s1_send.at[slot], r2_recv.at[j],
                    (row, col, jnp.where(low, 2, 1)))

    def s3(j):
        slot = lax.rem(j, RING)
        return push(part.at[slot, :, at_rows(0, 3 * own, own)], r2.at[j, :, pl.ds(0, own)], s2_send.at[slot], r2_recv.at[j],
                    (row, col, jnp.where(low, 0, 3)))

    def sent(j):
        @pl.when(end)
        def _():
            s1(j).wait_send()

        @pl.when(jnp.logical_not(end))
        def _():
            s2(j).wait_send()
            s3(j).wait_send()

    own_copy = pltpu.make_async_copy(grad, every.at[pl.ds(pl.multiple_of(rows_of(row, z), 16), own)], g_local.at[0])
    own_copy.start()
    place = pl.ds(pl.multiple_of(in_half * local_rows, 8), local_rows)
    hop = push(tokens, tok.at[2, place], tok_send.at[0], tok_recv.at[0], peers[2])
    keep = pltpu.make_async_copy(tokens, tok.at[0, place], tok_local.at[0])

    @pl.when(jnp.logical_not(holds))
    def _():
        hop.start()

    def fan(i, m):
        to = (row, lax.rem(col + i, cols), z)
        src = tokens if m == 0 else tok.at[2, place]
        return push(src, tok.at[2 * m, place], fan_send.at[m, i], fan_recv.at[m, in_half], to)

    @pl.when(holds)
    def _():
        keep.start()

        @pl.loop(1, cols)
        def _(i):
            fan(i, 0).start()

    w_copy(1, 0).start()
    w_copy(2, 0).start()
    w_copy(3, 0).start()
    c_copy().start()
    for q in range(PREFILL):
        g_step(0, q)

    @pl.loop(1, min(AHEAD, n))
    def _(j):
        for m in (1, 2, 3):
            w_copy(m, j).start()

    @pl.when(holds)
    def _():
        hop.wait_recv()

        @pl.loop(1, cols)
        def _(i):
            fan(i, 1).start()
        keep.wait()

    @pl.loop(0, group)
    def _(i):
        other = pl.ds(pl.multiple_of(i * local_rows, 8), local_rows)

        @pl.when(jnp.logical_or(jnp.logical_not(holds), i != in_half))
        def _():
            for m in (0, 1):
                push(tokens, tok.at[2 * m, other], fan_send.at[m, 0], fan_recv.at[m, i], (row, col, z)).wait_recv()

    pairs = [push(tok.at[2 * m], tok.at[2 * m + 1], tok_send.at[1 + m], tok_recv.at[1 + m], peers[1]) for m in (0, 1)]
    for copy in pairs:
        copy.start()
    w_arrive(0)
    for copy in pairs:
        copy.wait_recv()

    depth = weight.shape[0]
    total = max(n + 4, 4 * per_stage - PREFILL)

    @pl.loop(0, total)
    def _(t):
        @pl.when(t < n)
        def _():
            @pl.when(t >= RING)
            def _():
                sent(t - RING)
            for copy in w_loads(t):
                copy.wait()
            slot, ws = lax.rem(t, RING), lax.rem(t, 2)

            @pl.loop(0, 2)
            def _(h):
                rows = pl.ds(pl.multiple_of(h * 4 * own, own), 4 * own)
                acc = jnp.dot(tok[0, rows], wslot[ws, pl.ds(0, depth)], preferred_element_type=jnp.float32)
                for m in (1, 2, 3):
                    acc += jnp.dot(tok[m, rows], wslot[ws, pl.ds(m * depth, depth)], preferred_element_type=jnp.float32)
                part[slot, h] = acc

            @pl.when(end)
            def _():
                s1(t).start()

            @pl.when(t + AHEAD < n)
            def _():
                for m in (1, 2, 3):
                    w_copy(m, t + AHEAD).start()

            @pl.when(t + 1 < n)
            def _():
                w_arrive(t + 1)

        @pl.when(jnp.logical_not(end) & (t >= 1) & (t - 1 < n))
        def _():
            j = t - 1
            slot = lax.rem(j, RING)
            s1(j).wait_recv()
            rows = at_rows(2 * own, 0, 2 * own)
            part[slot, :, rows] = part[slot, :, rows] + r1[j, :, at_rows(own, 0, 2 * own)]
            s2(j).start()

        @pl.when(jnp.logical_not(end) & (t >= 2) & (t - 2 < n))
        def _():
            j = t - 2
            slot = lax.rem(j, RING)
            s2(j).wait_recv()
            rows = at_rows(0, 3 * own, own)
            part[slot, :, rows] = part[slot, :, rows] + r2[j, :, at_rows(0, own, own)]
            s3(j).start()
            mine = part[slot, :, at_rows(own, 2 * own, own)]
            finish(j, mine + r1[j, :, at_rows(0, 2 * own, own)] + r2[j, :, at_rows(own, 0, own)])

        @pl.when(end & (t >= 4) & (t - 4 < n))
        def _():
            j = t - 4
            s3(j).wait_recv()
            finish(j, part[lax.rem(j, RING), :, at_rows(0, 3 * own, own)] + r2[j, :, pl.ds(0, own)])

        p = t + PREFILL
        for q in range(PIECES + 1):
            if q >= PREFILL:
                @pl.when(p == q)
                def _():
                    if q == PIECES:
                        c_landed().wait_recv()
                    g_step(0, q)
            for s in (1, 2, 3):
                @pl.when(p == s * per_stage + q)
                def _():
                    g_step(s, q)
                    if q == PIECES:
                        stage_done(s)

        @pl.when(t == 2)
        def _():
            own_copy.wait()
            block_done(z)

    for i in range(4):
        x_wait(i, i)
        d_copy(over, i, 4 + i).start()

    @pl.loop(max(0, n - RING), n)
    def _(j):
        sent(j)

    @pl.loop(max(0, n - 4), n)
    def _(j):
        o_wait(j)

    @pl.loop(0, n)
    def _(j):
        o_landed(j)
        for m in (1, 2, 3):
            w_copy(m, j).wait_send()

    for way in (0, 1):
        @pl.when(sends(way))
        def _():
            for q in range(PIECES):
                g_own(way, q).wait_send()
            g_copy(way, 0, PIECES, True).wait_send()
        for s in (1, 2, 3):
            @pl.when(has(way, s) & sends(way))
            def _():
                for q in range(PIECES + 1):
                    g_copy(way, s, q, True).wait_send()
    c_copy().wait_send()
    for i in range(4):
        x_copy(i, i).wait_send()
        d_copy(row, i, i).wait_send()
        d_copy(over, i, 4 + i).wait_send()
        d_copy(near, i, i).wait_recv()
        d_copy(cross, i, 4 + i).wait_recv()

    @pl.when(jnp.logical_not(holds))
    def _():
        hop.wait_send()

    @pl.when(holds)
    def _():
        @pl.loop(1, cols)
        def _(i):
            fan(i, 0).wait_send()
            fan(i, 1).wait_send()
    for copy in pairs:
        copy.wait_send()


def local(cols, tokens, weight, prev_tokens, prev_grad):
    depth, width = weight.shape
    half = width // 2
    n = half // CC
    own = prev_grad.shape[0]
    carry = own * 3 // 8
    dma = pltpu.SemaphoreType.DMA
    anywhere = pl.BlockSpec(memory_space=pl.ANY)
    qkv, every, _ = pl.pallas_call(
        functools.partial(kernel, n, cols, carry),
        out_shape=(
            jax.ShapeDtypeStruct((own, width), jnp.bfloat16),
            jax.ShapeDtypeStruct((16 * own, width), jnp.bfloat16),
            jax.ShapeDtypeStruct((n, 3, depth, CC), jnp.bfloat16),
        ),
        in_specs=[anywhere] * 3,
        out_specs=(anywhere,) * 3,
        scratch_shapes=[
            pltpu.VMEM((4, 8 * own, depth), jnp.bfloat16),
            pltpu.VMEM((2, 4 * depth, CC), jnp.bfloat16),
            pltpu.VMEM((RING, 2, 4 * own, CC), jnp.float32),
            pltpu.VMEM((n, 2, 3 * own, CC), jnp.float32),
            pltpu.VMEM((n, 2, 2 * own, CC), jnp.float32),
            pltpu.VMEM((4, 2, own, CC), jnp.bfloat16),
            dma((1,)), dma((3,)), dma((3,)), dma((2, cols)), dma((2, cols // 2)),
            dma((3, n)), dma((3, n)), dma((2, 4)),
            dma((RING,)), dma((RING,)), dma((n,)), dma((n,)),
            dma((4,)), dma((4,)), dma((n,)),
            dma((2, 4 * (PIECES + 1))), dma((2, 4 * (PIECES + 1))), dma((1,)), dma((1,)), dma((1,)), dma((4,)), dma((4,)), dma((8,)), dma((8,)),
        ],
        compiler_params=pltpu.CompilerParams(has_side_effects=True, vmem_limit_bytes=64 * 1024 * 1024 - 65536),
        name="exchange",
    )(tokens, weight, prev_grad)
    prev_gathered = lax.all_gather(prev_tokens, "col", axis=0, tiled=True)
    weight_grad = lax.dot_general(prev_gathered, every, (((0,), (0,)), ((), ())), preferred_element_type=jnp.float32)
    return (qkv, weight_grad)


def solution(mesh):
    placed = (
        P("col", ("row", "depth")),
        P(("row", "depth"), "col"),
        P("col", ("row", "depth")),
        P(("row", "depth"), "col"),
    )
    cols = mesh.shape["col"]
    fits = mesh.shape["row"] == 4 and mesh.shape["depth"] == 4 and cols % 2 == 0
    return jax.shard_map(
        functools.partial(local, cols) if fits else plain,
        mesh=mesh,
        in_specs=placed,
        out_specs=(P(("row", "depth"), "col"), P(("row", "depth"), "col")),
        check_vma=False,
    )
```

time: 1070 us -> 690 us (0.64); the launches traced: 1070 us -> 679 us
  waiting for transfers between devices: 945 us -> 0.7 us
  Pallas kernels: 0 us -> 601 us
  matrix products: 73.5 us -> 36.5 us
  blocking collectives: 33.6 us -> 0 us
  local copies, waits for them, and re-layouts: 2.35 us -> 26.5 us
    pallas_call x0 -> x1, Pallas kernels: none -> 601 us  [local(): pl.pallas_call(functools.partial(kernel, n, cols, carry), out_shape=(jax....]
    all_gather x3 -> x0, waiting for transfers between devices: 563 us -> none  [the longest x1 267 us: local(): rows_of_weight = lax.all_gather(weight, 'row', axis=0, tiled=True)]
    reduce_scatter x1 -> x0, waiting for transfers between devices: 380 us -> none  [local(): lax.psum_scatter(jnp.dot(mine, rows_of_weight, preferred_element_type=jnp...]
    dot_general x2 -> x1, matrix products: 73.5 us -> 36.5 us  [local(): lax.dot_general(prev_gathered, every, (((0,), (0,)), ((), ())), preferred...]
    all_to_all x1 -> x0, blocking collectives: 33.6 us -> none  [local(): lax.all_to_all(gathered, 'row', split_axis=0, concat_axis=1, tiled=True)]
    unnamed x0 -> x4, local copies, waits for them, and re-layouts: none -> 26.5 us
  transfers between devices with their start and end apart: 5 -> 1, of which waited for: 4 -> 0; matrix products, arithmetic and copies ran while one was open for 7% -> 0% of each run, Pallas kernels for 0% -> 89%
where the time goes in v1:
time: 690 us; the launch traced here: 679 us
  Pallas kernels  601 us (87%)
  matrix products  36.5 us (5%)
  local copies, waits for them, and re-layouts  26.5 us (4%)
  between operations  14 us (2%)
    pallas_call x1, Pallas kernels, local(): pl.pallas_call(functools.partial(kernel, n, cols, carry), out_shape=(jax....  601 us
    dot_general x1, matrix products, local(): lax.dot_general(prev_gathered, every, (((0,), (0,)), ((), ())), preferred...  36.5 us
    unnamed x4, local copies, waits for them, and re-layouts  26.5 us
  transfers between devices with their start and end apart: 1, of which 0 were waited for; matrix products, arithmetic and copies ran while one was open for 0% of the time, Pallas kernels for 89%

profile of v1, /device:TPU:0, one launch (start us, length us, event | category | flops | bytes accessed | tf_op | source)
XLA Modules:
  0.0 679.0 jit_solution(12078732475348126323)
XLA Ops:
  7.2 0.0 all-gather.2.cloned.1.call-start
  7.2 0.7 all-gather.2.cloned.1.call-update
  7.9 601.2 %exchange.1 = (bf16[128,12288]{1,0:T(8,128)(2,1)}, bf16[2048,12288]{1,0:T(8,128)(2,1)}, bf16[24,3,512,256]{3,2,1,0:T(8,128)(2,1)}) custom-call(bf16[1024,512]{1,0:T(8,128)(2,1)} %tokens.1, bf16[512,12288]{1,0:T(8,128)(2,1)} %weight.1, bf16[128,12288]{1,0:T(8,128)(2,1)} %grad.1), custom_call_target="tpu_custom_call" | custom-call | tf_op jit(solution)/shard_map/exchange/pallas_call | solution.py:433
  609.1 0.0 all-gather.2.cloned.1.call-done
  609.1 36.5 %convolution_bitcast_fusion = f32[512,12288]{0,1:T(8,128)} fusion(bf16[2048,12288]{1,0:T(8,128)(2,1)} %get-tuple-element.5, bf16[2048,512]{1,0:T(8,128)(2,1)} %all-gather.2.cloned.1.call-done), kind=kOutput, calls=%fused_computation | convolution fusion | flops 25769803776 | bytes 77594624 | tf_op jit(solution)/shard_map/dot_general | solution.py:459
  645.6 0.0 copy-start
  645.6 24.8 %copy.6 = f32[512,12288]{1,0:T(8,128)} copy(f32[512,12288]{0,1:T(8,128)} %convolution_bitcast_fusion) | data formatting | bytes 50331648
  670.5 0.0 copy-done
  670.5 1.7 copy.8
Async XLA Ops:
  7.2 602.0 %all-gather.2.cloned.1.call-start = ((), (), s32[]{:S(2)}) async-start(), calls=%async_computation | async-start | bytes 3145728 | tf_op jit(solution)/shard_map/all_gather | solution.py:458
  645.6 24.8 %copy-start = (bf16[128,12288]{1,0:T(8,128)(2,1)S(1)}, bf16[128,12288]{1,0:T(8,128)(2,1)}, u32[]{:S(2)}) copy-start(bf16[128,12288]{1,0:T(8,128)(2,1)} %get-tuple-element.10) | copy-start | bytes 9437188
Sparse Core Ops, SparseCore 0:
  9.5 56.0 all-gather.1

commit v2 on v1

--- a/solution.py
+++ b/solution.py
@@ -1,4 +1,5 @@
 import functools
+import math
 
 import jax
 import jax.numpy as jnp
@@ -12,6 +13,7 @@
 RING = 8
 PREFILL = 3
 PIECES = 4
+LATE, GAP = 13, 3
 MESH = pl.DeviceIdType.MESH
 
 
@@ -37,14 +39,15 @@
 
 def kernel(
     n, cols, carry,
-    tokens, weight, grad,
-    qkv, every, spread,
+    tokens, weight, prev, grad,
+    qkv, every, prev_all, spread,
     tok, wslot, part, r1, r2, out,
     tok_local, tok_send, tok_recv, fan_send, fan_recv,
     w_send, w_recv, w_local,
     s1_send, s2_send, r1_recv, r2_recv,
     o_local, o_send, o_recv,
     g_send, g_recv, g_local, c_send, c_recv, x_send, x_recv, d_send, d_recv,
+    p_local, p_send, p_recv,
 ):
     row, col, z = lax.axis_index("row"), lax.axis_index("col"), lax.axis_index("depth")
     x, core = row // 2, row % 2
@@ -176,6 +179,18 @@
             def _():
                 block_done(z - step * s)
 
+    def crossed(d):
+        x_wait(d, d)
+        d_copy(over, d, 4 + d).start()
+
+    def crossed_stage(s):
+        for way in (0, 1):
+            step = 1 - 2 * way
+
+            @pl.when(has(way, s))
+            def _():
+                crossed(z - step * s)
+
     def o_copies(j):
         slot = lax.rem(j, 4)
         at = pl.multiple_of(core * half + j * CC, CC)
@@ -257,7 +272,7 @@
     w_copy(2, 0).start()
     w_copy(3, 0).start()
     c_copy().start()
-    for q in range(PREFILL):
+    for q in range(min(PREFILL, PIECES)):
         g_step(0, q)
 
     @pl.loop(1, min(AHEAD, n))
@@ -274,6 +289,10 @@
             fan(i, 1).start()
         keep.wait()
 
+    if PREFILL > PIECES:
+        c_landed().wait_recv()
+        g_step(0, PIECES)
+
     @pl.loop(0, group)
     def _(i):
         other = pl.ds(pl.multiple_of(i * local_rows, 8), local_rows)
@@ -282,6 +301,18 @@
         def _():
             for m in (0, 1):
                 push(tokens, tok.at[2 * m, other], fan_send.at[m, 0], fan_recv.at[m, i], (row, col, z)).wait_recv()
+
+    def p_copy(i):
+        to = (row, lax.rem(col + i, cols), z)
+        at = pl.ds(pl.multiple_of(col * local_rows, 8), local_rows)
+        return push(prev, prev_all.at[at], p_send.at[i], p_recv.at[col], to)
+
+    p_keep = pltpu.make_async_copy(prev, prev_all.at[pl.ds(pl.multiple_of(col * local_rows, 8), local_rows)], p_local.at[0])
+    p_keep.start()
+
+    @pl.loop(1, cols)
+    def _(i):
+        p_copy(i).start()
 
     pairs = [push(tok.at[2 * m], tok.at[2 * m + 1], tok_send.at[1 + m], tok_recv.at[1 + m], peers[1]) for m in (0, 1)]
     for copy in pairs:
@@ -291,7 +322,7 @@
         copy.wait_recv()
 
     depth = weight.shape[0]
-    total = max(n + 4, 4 * per_stage - PREFILL)
+    total = max(n + 4, 4 * per_stage - PREFILL, LATE + 2 * GAP + 1)
 
     @pl.loop(0, total)
     def _(t):
@@ -371,9 +402,24 @@
             own_copy.wait()
             block_done(z)
 
-    for i in range(4):
-        x_wait(i, i)
-        d_copy(over, i, 4 + i).start()
+        @pl.when(t == LATE)
+        def _():
+            crossed(z)
+        for s in (1, 2):
+            @pl.when(t == LATE + GAP * s)
+            def _():
+                crossed_stage(s)
+
+    p_keep.wait()
+
+    @pl.loop(1, cols)
+    def _(i):
+        source = lax.rem(col + i, cols)
+        at = pl.ds(pl.multiple_of(source * local_rows, 8), local_rows)
+        push(prev, prev_all.at[at], p_send.at[i], p_recv.at[source], (row, col, z)).wait_recv()
+        p_copy(i).wait_send()
+
+    crossed_stage(3)
 
     @pl.loop(max(0, n - RING), n)
     def _(j):
@@ -422,23 +468,28 @@
         copy.wait_send()
 
 
+def product(left, right, out):
+    out[...] = lax.dot_general(left[...], right[...], (((0,), (0,)), ((), ())), preferred_element_type=jnp.float32)
+
+
 def local(cols, tokens, weight, prev_tokens, prev_grad):
     depth, width = weight.shape
     half = width // 2
     n = half // CC
     own = prev_grad.shape[0]
-    carry = own * 3 // 8
+    carry = own // 4
     dma = pltpu.SemaphoreType.DMA
     anywhere = pl.BlockSpec(memory_space=pl.ANY)
-    qkv, every, _ = pl.pallas_call(
+    qkv, every, prev_all, _ = pl.pallas_call(
         functools.partial(kernel, n, cols, carry),
         out_shape=(
             jax.ShapeDtypeStruct((own, width), jnp.bfloat16),
             jax.ShapeDtypeStruct((16 * own, width), jnp.bfloat16),
+            jax.ShapeDtypeStruct((8 * own * 2, depth), jnp.bfloat16),
             jax.ShapeDtypeStruct((n, 3, depth, CC), jnp.bfloat16),
         ),
-        in_specs=[anywhere] * 3,
-        out_specs=(anywhere,) * 3,
+        in_specs=[anywhere] * 4,
+        out_specs=(anywhere,) * 4,
         scratch_shapes=[
             pltpu.VMEM((4, 8 * own, depth), jnp.bfloat16),
             pltpu.VMEM((2, 4 * depth, CC), jnp.bfloat16),
@@ -451,12 +502,21 @@
             dma((RING,)), dma((RING,)), dma((n,)), dma((n,)),
             dma((4,)), dma((4,)), dma((n,)),
             dma((2, 4 * (PIECES + 1))), dma((2, 4 * (PIECES + 1))), dma((1,)), dma((1,)), dma((1,)), dma((4,)), dma((4,)), dma((8,)), dma((8,)),
+            dma((1,)), dma((cols,)), dma((cols,)),
         ],
         compiler_params=pltpu.CompilerParams(has_side_effects=True, vmem_limit_bytes=64 * 1024 * 1024 - 65536),
         name="exchange",
-    )(tokens, weight, prev_grad)
-    prev_gathered = lax.all_gather(prev_tokens, "col", axis=0, tiled=True)
-    weight_grad = lax.dot_general(prev_gathered, every, (((0,), (0,)), ((), ())), preferred_element_type=jnp.float32)
+    )(tokens, weight, prev_tokens, prev_grad)
+    tile = math.gcd(width, 1536)
+    weight_grad = pl.pallas_call(
+        product,
+        out_shape=jax.ShapeDtypeStruct((depth, width), jnp.float32),
+        grid=(width // tile,),
+        in_specs=[pl.BlockSpec((16 * own, depth), lambda i: (0, 0)), pl.BlockSpec((16 * own, tile), lambda i: (0, i))],
+        out_specs=pl.BlockSpec((depth, tile), lambda i: (0, i)),
+        compiler_params=pltpu.CompilerParams(vmem_limit_bytes=32 * 1024 * 1024),
+        name="product",
+    )(prev_all, every)
     return (qkv, weight_grad)
 
 

time: 690 us -> 614 us (0.89); the launches traced: 679 us -> 613 us
  matrix products: 36.5 us -> 0 us
  local copies, waits for them, and re-layouts: 26.5 us -> 3.25 us
  between operations: 14 us -> 0.65 us
  Pallas kernels: 601 us -> 609 us
    dot_general x1 -> x0, matrix products: 36.5 us -> none  [local(): lax.dot_general(prev_gathered, every, (((0,), (0,)), ((), ())), preferred...]
    pallas_call x0 -> x1, Pallas kernels: none -> 33.9 us  [local(): pl.pallas_call(product, out_shape=jax.ShapeDtypeStruct((depth, width), jn...]
    pallas_call x1, Pallas kernels: 601 us -> 575 us  [local(): pl.pallas_call(functools.partial(kernel, n, cols, carry), out_shape=(jax....]
    unnamed x4 -> x5, local copies, waits for them, and re-layouts: 26.5 us -> 3.25 us
  transfers between devices with their start and end apart: 1 -> 0, of which waited for: 0 -> 0; matrix products, arithmetic and copies ran while one was open for 0% -> 0% of each run, Pallas kernels for 89% -> 0%
where the time goes in v2:
time: 614 us; the launch traced here: 613 us
  Pallas kernels  609 us (99%)
    pallas_call x1, Pallas kernels, local(): pl.pallas_call(functools.partial(kernel, n, cols, carry), out_shape=(jax....  575 us
    pallas_call x1, Pallas kernels, local(): pl.pallas_call(product, out_shape=jax.ShapeDtypeStruct((depth, width), jn...  33.9 us

profile of v2, /device:TPU:0, one launch (start us, length us, event | category | flops | bytes accessed | tf_op | source)
XLA Modules:
  0.0 613.1 jit_solution(3979950290652371323)
XLA Ops:
  0.6 575.3 %exchange.1 = (bf16[128,12288]{1,0:T(8,128)(2,1)}, bf16[2048,12288]{1,0:T(8,128)(2,1)}, bf16[2048,512]{1,0:T(8,128)(2,1)}, bf16[24,3,512,256]{3,2,1,0:T(8,128)(2,1)}) custom-call(bf16[1024,512]{1,0:T(8,128)(2,1)} %tokens.1, bf16[512,12288]{1,0:T(8,128)(2,1)} %weight.1, bf16[1024,512]{1,0:T(8,128)(2,1)} %prev.1, bf16[128,12288]{1,0:T(8,128)(2,1)} %grad.1), custom_call_target="tpu_custom_call" | custom-call | tf_op jit(solution)/shard_map/exchange/pallas_call | solution.py:483
  575.9 0.0 copy-start
  575.9 1.6 copy-done
  577.5 0.0 copy-start.1
  577.5 33.9 %product.1 = f32[512,12288]{1,0:T(8,128)} custom-call(bf16[2048,512]{1,0:T(8,128)(2,1)S(1)} %copy-done, bf16[2048,12288]{1,0:T(8,128)(2,1)} %get-tuple-element.7.right), custom_call_target="tpu_custom_call" | custom-call | tf_op jit(solution)/shard_map/product/pallas_call | solution.py:511
  611.4 0.0 copy-done.1
  611.4 1.7 copy.7
Async XLA Ops:
  575.9 1.6 copy-start
  577.5 33.9 %copy-start.1 = (bf16[128,12288]{1,0:T(8,128)(2,1)S(1)}, bf16[128,12288]{1,0:T(8,128)(2,1)}, u32[]{:S(2)}) copy-start(bf16[128,12288]{1,0:T(8,128)(2,1)} %get-tuple-element.10) | copy-start | bytes 9437188

commit v3 on v2

--- a/solution.py
+++ b/solution.py
@@ -11,9 +11,12 @@
 CC = 256
 AHEAD = 8
 RING = 8
-PREFILL = 3
+PREFILL = 5
+STEPS = 10
+SCALE = 256 * (STEPS + 0.5)
 PIECES = 4
-LATE, GAP = 13, 3
+LATE, GAP = 20, 5
+REST = 3
 MESH = pl.DeviceIdType.MESH
 
 
@@ -37,14 +40,32 @@
     return (summed.astype(jnp.bfloat16), weight_grad)
 
 
+def code(ref, value):
+    head = value.astype(jnp.bfloat16)
+    wide = head.astype(jnp.float32)
+    steps = jnp.round((value - wide) * SCALE / jnp.where(wide == 0, 1.0, wide))
+    steps = jnp.clip(steps, -STEPS, STEPS)
+    half = CC // 2
+    ref[:, pl.ds(0, CC)] = head
+    ref[:, pl.ds(CC, half)] = ((2 * STEPS + 1) * steps[:, :half] + steps[:, half:]).astype(jnp.bfloat16)
+
+
+def decode(coded):
+    head = coded[..., :CC].astype(jnp.float32)
+    both = coded[..., CC:].astype(jnp.float32)
+    upper = jnp.round(both * (1 / (2 * STEPS + 1)))
+    steps = jnp.concatenate([upper, both - (2 * STEPS + 1) * upper], -1)
+    return head + head * steps * (1 / SCALE)
+
+
 def kernel(
     n, cols, carry,
     tokens, weight, prev, grad,
     qkv, every, prev_all, spread,
-    tok, wslot, part, r1, r2, out,
+    tok, wslot, part, first, second, r1, r2, r3, out,
     tok_local, tok_send, tok_recv, fan_send, fan_recv,
     w_send, w_recv, w_local,
-    s1_send, s2_send, r1_recv, r2_recv,
+    s1_send, s2_send, r1_recv, r2_recv, r3_recv,
     o_local, o_send, o_recv,
     g_send, g_recv, g_local, c_send, c_recv, x_send, x_recv, d_send, d_recv,
     p_local, p_send, p_recv,
@@ -222,17 +243,17 @@
 
     def s1(j):
         slot = lax.rem(j, RING)
-        return push(part.at[slot, :, at_rows(own, 0, 3 * own)], r1.at[j], s1_send.at[slot], r1_recv.at[j],
+        return push(first.at[slot], r1.at[j], s1_send.at[slot], r1_recv.at[j],
                     (row, col, jnp.where(low, 1, 2)))
 
     def s2(j):
         slot = lax.rem(j, RING)
-        return push(part.at[slot, :, at_rows(2 * own, 0, 2 * own)], r2.at[j], s1_send.at[slot], r2_recv.at[j],
+        return push(second.at[slot], r2.at[j], s1_send.at[slot], r2_recv.at[j],
                     (row, col, jnp.where(low, 2, 1)))
 
     def s3(j):
         slot = lax.rem(j, RING)
-        return push(part.at[slot, :, at_rows(0, 3 * own, own)], r2.at[j, :, pl.ds(0, own)], s2_send.at[slot], r2_recv.at[j],
+        return push(part.at[slot, :, at_rows(0, 3 * own, own)], r3.at[j], s2_send.at[slot], r3_recv.at[j],
                     (row, col, jnp.where(low, 0, 3)))
 
     def sent(j):
@@ -322,7 +343,7 @@
         copy.wait_recv()
 
     depth = weight.shape[0]
-    total = max(n + 4, 4 * per_stage - PREFILL, LATE + 2 * GAP + 1)
+    total = max(n + 4, REST * -(-(4 * per_stage - PREFILL) // (REST - 1)), LATE + GAP + 1)
 
     @pl.loop(0, total)
     def _(t):
@@ -345,6 +366,11 @@
 
             @pl.when(end)
             def _():
+                @pl.loop(0, 2 * 3)
+                def _(i):
+                    h, g = i // 3, i % 3
+                    value = part[slot, h, pl.ds(pl.multiple_of(jnp.where(low, own, 0) + g * own, own), own)]
+                    code(first.at[slot, h, pl.ds(pl.multiple_of(g * own, own), own)], value)
                 s1(t).start()
 
             @pl.when(t + AHEAD < n)
@@ -361,8 +387,13 @@
             j = t - 1
             slot = lax.rem(j, RING)
             s1(j).wait_recv()
-            rows = at_rows(2 * own, 0, 2 * own)
-            part[slot, :, rows] = part[slot, :, rows] + r1[j, :, at_rows(own, 0, 2 * own)]
+
+            @pl.loop(0, 2 * 2)
+            def _(i):
+                h, g = i // 2, i % 2
+                value = part[slot, h, pl.ds(pl.multiple_of(jnp.where(low, 2 * own, 0) + g * own, own), own)]
+                value += decode(r1[j, h, pl.ds(pl.multiple_of(jnp.where(low, own, 0) + g * own, own), own)])
+                code(second.at[slot, h, pl.ds(pl.multiple_of(g * own, own), own)], value)
             s2(j).start()
 
         @pl.when(jnp.logical_not(end) & (t >= 2) & (t - 2 < n))
@@ -371,18 +402,19 @@
             slot = lax.rem(j, RING)
             s2(j).wait_recv()
             rows = at_rows(0, 3 * own, own)
-            part[slot, :, rows] = part[slot, :, rows] + r2[j, :, at_rows(0, own, own)]
+            part[slot, :, rows] = part[slot, :, rows] + decode(r2[j, :, at_rows(0, own, own)])
             s3(j).start()
             mine = part[slot, :, at_rows(own, 2 * own, own)]
-            finish(j, mine + r1[j, :, at_rows(0, 2 * own, own)] + r2[j, :, at_rows(own, 0, own)])
+            finish(j, mine + decode(r1[j, :, at_rows(0, 2 * own, own)]) + decode(r2[j, :, at_rows(own, 0, own)]))
 
         @pl.when(end & (t >= 4) & (t - 4 < n))
         def _():
             j = t - 4
             s3(j).wait_recv()
-            finish(j, part[lax.rem(j, RING), :, at_rows(0, 3 * own, own)] + r2[j, :, pl.ds(0, own)])
-
-        p = t + PREFILL
+            finish(j, part[lax.rem(j, RING), :, at_rows(0, 3 * own, own)] + r3[j])
+
+        turn = lax.rem(t, REST)
+        p = jnp.where(turn < REST - 1, PREFILL + (REST - 1) * (t // REST) + turn, -1)
         for q in range(PIECES + 1):
             if q >= PREFILL:
                 @pl.when(p == q)
@@ -405,10 +437,10 @@
         @pl.when(t == LATE)
         def _():
             crossed(z)
-        for s in (1, 2):
-            @pl.when(t == LATE + GAP * s)
-            def _():
-                crossed_stage(s)
+
+        @pl.when(t == LATE + GAP)
+        def _():
+            crossed_stage(1)
 
     p_keep.wait()
 
@@ -419,6 +451,7 @@
         push(prev, prev_all.at[at], p_send.at[i], p_recv.at[source], (row, col, z)).wait_recv()
         p_copy(i).wait_send()
 
+    crossed_stage(2)
     crossed_stage(3)
 
     @pl.loop(max(0, n - RING), n)
@@ -477,7 +510,7 @@
     half = width // 2
     n = half // CC
     own = prev_grad.shape[0]
-    carry = own // 4
+    carry = own // 2
     dma = pltpu.SemaphoreType.DMA
     anywhere = pl.BlockSpec(memory_space=pl.ANY)
     qkv, every, prev_all, _ = pl.pallas_call(
@@ -494,12 +527,15 @@
             pltpu.VMEM((4, 8 * own, depth), jnp.bfloat16),
             pltpu.VMEM((2, 4 * depth, CC), jnp.bfloat16),
             pltpu.VMEM((RING, 2, 4 * own, CC), jnp.float32),
-            pltpu.VMEM((n, 2, 3 * own, CC), jnp.float32),
-            pltpu.VMEM((n, 2, 2 * own, CC), jnp.float32),
+            pltpu.VMEM((RING, 2, 3 * own, CC * 3 // 2), jnp.bfloat16),
+            pltpu.VMEM((RING, 2, 2 * own, CC * 3 // 2), jnp.bfloat16),
+            pltpu.VMEM((n, 2, 3 * own, CC * 3 // 2), jnp.bfloat16),
+            pltpu.VMEM((n, 2, 2 * own, CC * 3 // 2), jnp.bfloat16),
+            pltpu.VMEM((n, 2, own, CC), jnp.float32),
             pltpu.VMEM((4, 2, own, CC), jnp.bfloat16),
             dma((1,)), dma((3,)), dma((3,)), dma((2, cols)), dma((2, cols // 2)),
             dma((3, n)), dma((3, n)), dma((2, 4)),
-            dma((RING,)), dma((RING,)), dma((n,)), dma((n,)),
+            dma((RING,)), dma((RING,)), dma((n,)), dma((n,)), dma((n,)),
             dma((4,)), dma((4,)), dma((n,)),
             dma((2, 4 * (PIECES + 1))), dma((2, 4 * (PIECES + 1))), dma((1,)), dma((1,)), dma((1,)), dma((4,)), dma((4,)), dma((8,)), dma((8,)),
             dma((1,)), dma((cols,)), dma((cols,)),

time: 614 us -> 563 us (0.917)
  Pallas kernels: 609 us -> 558 us
    pallas_call x1, Pallas kernels: 575 us -> 525 us  [local(): pl.pallas_call(functools.partial(kernel, n, cols, carry), out_shape=(jax....]
where the time goes in v3:
time: 563 us; the launch traced here: 562 us
  Pallas kernels  558 us (99%)
    pallas_call x1, Pallas kernels, local(): pl.pallas_call(functools.partial(kernel, n, cols, carry), out_shape=(jax....  525 us
    pallas_call x1, Pallas kernels, local(): pl.pallas_call(product, out_shape=jax.ShapeDtypeStruct((depth, width), jn...  33.9 us

profile of v3, /device:TPU:0, one launch (start us, length us, event | category | flops | bytes accessed | tf_op | source)
XLA Modules:
  0.0 562.3 jit_solution(1188047172445831091)
XLA Ops:
  0.6 524.5 %exchange.1 = (bf16[128,12288]{1,0:T(8,128)(2,1)}, bf16[2048,12288]{1,0:T(8,128)(2,1)}, bf16[2048,512]{1,0:T(8,128)(2,1)}, bf16[24,3,512,256]{3,2,1,0:T(8,128)(2,1)}) custom-call(bf16[1024,512]{1,0:T(8,128)(2,1)} %tokens.1, bf16[512,12288]{1,0:T(8,128)(2,1)} %weight.1, bf16[1024,512]{1,0:T(8,128)(2,1)} %prev.1, bf16[128,12288]{1,0:T(8,128)(2,1)} %grad.1), custom_call_target="tpu_custom_call" | custom-call | tf_op jit(solution)/shard_map/exchange/pallas_call | solution.py:516
  525.2 0.0 copy-start
  525.2 1.6 copy-done
  526.7 0.0 copy-start.1
  526.7 33.9 %product.1 = f32[512,12288]{1,0:T(8,128)} custom-call(bf16[2048,512]{1,0:T(8,128)(2,1)S(1)} %copy-done, bf16[2048,12288]{1,0:T(8,128)(2,1)} %get-tuple-element.7.right), custom_call_target="tpu_custom_call" | custom-call | tf_op jit(solution)/shard_map/product/pallas_call | solution.py:547
  560.6 0.0 copy-done.1
  560.6 1.7 copy.7
Async XLA Ops:
  525.2 1.6 copy-start
  526.7 33.9 %copy-start.1 = (bf16[128,12288]{1,0:T(8,128)(2,1)S(1)}, bf16[128,12288]{1,0:T(8,128)(2,1)}, u32[]{:S(2)}) copy-start(bf16[128,12288]{1,0:T(8,128)(2,1)} %get-tuple-element.10) | copy-start | bytes 9437188
